TPU v7x, 512 devices: a whole 4x4x16 slice. The times are simulated.
512 devices in a mesh: box: 16 (over x, y_hi, core), sib: 2 (over y_lo), grp: 16 (over z).
Axes of the slice: x: 4, y: 4 (y_hi: 2, y_lo: 2; y = y_hi * 2 + y_lo), z: 16, core: 2. Of those that a mesh axis runs over, the one named last changes fastest.
Arguments:
- interface_maps: float32 [2, 32, 1024, 1024], P('sib', 'box', 'grp'), parts along dimension 1, may hold values from -1 to 1
- pivot_inverses: float32 [2, 32, 512, 512], P('sib', 'box', None, 'grp'), parts along dimension 1, may hold values from -1 to 5
- exterior_coupling: float32 [32, 1024, 5120], P('box', 'sib', 'grp'), parts along dimension 0, may hold values from -1 to 1
- face_blocks: int32 [32, 8], P('box'), parts along dimension 0, may hold values from 0 to 7, each once within a row
Outputs:
- interface_schur: float32 [32, 1024, 1024], P('box', 'sib', 'grp'), parts along dimension 0
- exterior_update: float32 [32, 1024, 5120], P('box', 'sib', 'grp'), parts along dimension 0
- multipliers: float32 [32, 1024, 1024], P('box', 'grp', 'sib'), parts along dimension 0
There are 16 independent parts, one for each index of `box`. A program takes and returns all parts, laid end to end along the dimension named above; each array names one. Nothing has to cross between parts.
Inputs may be any that keep to these rules, and one draw needn't show every extreme that they name: `face_blocks`: each row is an ordering of the 8 blocks of one child: row 0 for the first child, row 1 for the second.
All inputs are finite; a program needn't handle non-finite values.
Results may differ from a plain program's by a relative error of at most 0.0001.
Values sent between devices are 32-bit elements; how exact they have to be, the bound alone decides.
A program may use at most 128 MiB of HBM per device.

v0:
```python
import jax
import jax.numpy as jnp
from jax import lax
from jax.sharding import PartitionSpec as P


def partner(block, axis, bit):
    count = lax.axis_size(axis)
    route = []
    for low in range(count):
        high = low | 1 << bit
        if high != low and high < count:
            route += [(low, high), (high, low)]
    return lax.ppermute(block, axis, route)


def in_blocks(shard, dim, count):
    dims = shard.shape
    pieces = shard.reshape(*dims[:dim], count, dims[dim] // count, *dims[dim + 1 :])
    return jnp.moveaxis(pieces, dim, 0)


def summed_on_arrival(shard, axis, dim):
    pieces = in_blocks(shard, dim, lax.axis_size(axis))
    arrived = lax.all_to_all(pieces, axis, split_axis=0, concat_axis=0, tiled=True)
    return arrived.sum(axis=0)


def in_one_piece(arrays, axis, dim, along):
    ends, at = ([], 0)
    for a in arrays[:-1]:
        at += a.shape[along]
        ends.append(at)
    both = jnp.concatenate(arrays, axis=along)
    return tuple(jnp.split(summed_on_arrival(both, axis, dim), ends, axis=along))


def complex_dot(left_side, right_side):

    def product(first_part, second_part):
        return jnp.dot(
            first_part,
            second_part,
            precision=lax.Precision.HIGHEST,
            preferred_element_type=jnp.float32,
        )

    real_part = product(left_side[0], right_side[0]) - product(left_side[1], right_side[1])
    imag_part = product(left_side[0], right_side[1]) + product(left_side[1], right_side[0])
    return jnp.stack([real_part, imag_part])


def block_sources(face_blocks):
    alpha_order = face_blocks[0]
    beta_order = face_blocks[1]
    slots = jnp.arange(face_blocks.shape[1], dtype=jnp.int32)
    beta_match = (beta_order[:, None] == slots[None, :]).astype(jnp.int32)
    alpha_match = (alpha_order[:, None] == slots[None, :]).astype(jnp.int32)
    to_beta = jnp.sum(beta_match * alpha_order[:, None], axis=0)
    to_alpha = jnp.sum(alpha_match * beta_order[:, None], axis=0)
    return (to_beta, to_alpha)


def reorder(matrix, source):
    blocks = source.shape[0]
    grouped = matrix.reshape(matrix.shape[0], blocks, matrix.shape[1] // blocks, matrix.shape[2])
    return jnp.take(grouped, source, axis=1).reshape(matrix.shape)


def per_device(interface_maps, pivot_inverses, exterior_coupling, face_blocks):
    own_rows = interface_maps[0]
    partner_rows = partner(own_rows, "sib", 0)
    sibling = lax.axis_index("sib")
    member = lax.axis_index("grp")
    alpha_rows = jnp.where(sibling == 0, own_rows, partner_rows)
    beta_rows = jnp.where(sibling == 0, partner_rows, own_rows)
    local_rows = own_rows.shape[1]
    order_size = own_rows.shape[2]
    panel_width = pivot_inverses.shape[2]
    half_rows = order_size // 2
    to_beta, to_alpha = block_sources(face_blocks)
    panel_section = lax.dynamic_slice_in_dim(alpha_rows, sibling * panel_width, panel_width, 2)
    raw_multipliers = complex_dot(
        panel_section, lax.all_gather(pivot_inverses, "grp", axis=3, tiled=True)[0]
    )
    beta_cols = lax.all_to_all(beta_rows, "grp", split_axis=2, concat_axis=1, tiled=True)
    beta_perm = reorder(beta_cols, to_alpha)
    local_cols = beta_perm.shape[2]
    beta_panel = lax.dynamic_slice_in_dim(beta_perm, sibling * panel_width, panel_width, 1)
    piece = lax.all_gather(raw_multipliers, "grp", axis=1, tiled=True)
    joined = jnp.concatenate(
        [piece, -complex_dot(piece, beta_panel), complex_dot(piece, exterior_coupling)], axis=2
    )
    joined = reorder(joined, to_beta)
    multipliers = lax.dynamic_slice_in_dim(
        joined[:, :, :panel_width], member * local_rows, local_rows, 1
    )
    partial_schur = joined[:, :, panel_width : panel_width + local_cols]
    partial_exterior = joined[:, :, panel_width + local_cols :]
    summed_schur, exterior_update = in_one_piece((partial_schur, partial_exterior), "sib", 1, 2)
    row_index = sibling * half_rows + jnp.arange(half_rows, dtype=jnp.int32)
    col_index = member * local_cols + jnp.arange(local_cols, dtype=jnp.int32)
    identity_real = (row_index[:, None] == col_index[None, :]).astype(jnp.float32)
    identity_block = jnp.stack([identity_real, jnp.zeros_like(identity_real)])
    interface_schur = identity_block + summed_schur
    return (interface_schur, exterior_update, multipliers)


def solution(mesh):
    in_specs = (
        P("sib", "box", "grp", None),
        P("sib", "box", None, "grp"),
        P("box", "sib", "grp"),
        P("box", None),
    )
    out_specs = (P("box", "sib", "grp"), P("box", "sib", "grp"), P("box", "grp", "sib"))
    return jax.shard_map(
        per_device, mesh=mesh, in_specs=in_specs, out_specs=out_specs, check_vma=False
    )
```

profile of v0, /device:TPU:4, one launch (start us, length us, event | category | flops | bytes accessed | tf_op | source)
XLA Modules:
  0.0 277.3 jit_solution(12519139690456995614)
XLA Ops:
  7.2 0.7 all-gather.3.cloned.1.call-update
  7.9 3.5 %collective-permute-start = (f32[2,64,1024]{2,1,0:T(8,128)}, f32[2,64,1024]{2,1,0:T(8,128)S(1)}, u32[]{:S(2)}, u32[]{:S(2)}) collective-permute-start(f32[2,64,1024]{2,1,0:T(8,128)} %bitcast.121), channel_id=1, source_target_pairs={{0,16},{16,0},{1,17},{17,1},{2,18},{18,2},{3,19},{19,3},{4,20},{20... | collective-permute-start | bytes 1572872 | tf_op jit(solution)/shard_map/ppermute | solution.py:14
  11.4 12.3 %collective-permute-done = f32[2,64,1024]{2,1,0:T(8,128)S(1)} collective-permute-done((f32[2,64,1024]{2,1,0:T(8,128)}, f32[2,64,1024]{2,1,0:T(8,128)S(1)}, u32[]{:S(2)}, u32[]{:S(2)}) %collective-permute-start) | collective-permute-done | bytes 524320 | tf_op jit(solution)/shard_map/ppermute | solution.py:14
  23.7 1.0 dynamic-slice_select_fusion.1
  24.7 62.4 %all-gather.3.cloned.1.call-done = f32[1,2,512,512]{2,3,1,0:T(8,128)} async-done(((f32[1,2,512,32]{2,3,1,0:T(8,128)}), f32[1,2,512,512]{2,3,1,0:T(8,128)}) %all-gather.3.cloned.1.call-update) | async-done | bytes 2097168 | tf_op jit(solution)/shard_map/all_gather | solution.py:84
  87.1 2.5 fusion.19
  89.6 2.3 fusion.18
  91.9 1.1 fusion.17
  93.0 1.1 fusion.16
  94.2 0.7 pad_maximum_fusion.2
  95.0 0.6 copy.106
  95.6 1.9 reshape.137
  97.5 8.0 %all-to-all-start = ((f32[16,1,8192]{2,1,0:T(1,128)}), f32[16,1,8192]{2,1,0:T(1,128)S(1)}, u32[]{:S(2)}, u32[]{:S(2)}) async-start(f32[16,1,8192]{2,1,0:T(1,128)} %reshape.137), calls=%async_computation | async-start | bytes 1048576 | tf_op jit(solution)/shard_map/all_to_all | solution.py:86
  105.9 24.2 %all-to-all-done = f32[16,1,8192]{2,1,0:T(1,128)S(1)} async-done(((f32[16,1,8192]{2,1,0:T(1,128)}), f32[16,1,8192]{2,1,0:T(1,128)S(1)}, u32[]{:S(2)}, u32[]{:S(2)}) %all-to-all-start) | async-done | bytes 524320 | tf_op jit(solution)/shard_map/all_to_all | solution.py:86
  130.0 0.5 broadcast.132
  130.6 1.9 reduce
  132.5 0.8 reshape.138
  133.2 0.6 copy.123
  133.8 0.2 reshape.118
  134.2 0.6 gather_fusion
  134.8 43.9 %all-gather.5.cloned.1.call-done = f32[2,1024,512]{2,1,0:T(8,128)} async-done(((f32[2,64,512]{2,1,0:T(8,128)}), f32[2,1024,512]{2,1,0:T(8,128)}) %all-gather.5.cloned.1.call-update) | async-done | bytes 4194320 | tf_op jit(solution)/shard_map/all_gather | solution.py:90
  178.7 3.9 %fusion.3 = f32[1024,64]{0,1:T(8,128)S(1)} fusion(f32[2,1024,512]{2,1,0:T(8,128)} %all-gather.5.cloned.1.call-done, f32[2,512,64]{1,2,0:T(8,128)S(1)} %dynamic-slice_select_fusion), kind=kOutput, calls=%fused_computation.10 | convolution fusion | flops 402653184 | bytes 2490368 | tf_op jit(solution)/shard_map/dot_general | solution.py:41
  182.6 3.7 %fusion.2 = f32[1024,64]{0,1:T(8,128)S(1)} fusion(f32[2,1024,512]{2,1,0:T(8,128)} %all-gather.5.cloned.1.call-done, f32[2,512,64]{1,2,0:T(8,128)S(1)} %dynamic-slice_select_fusion), kind=kOutput, calls=%fused_computation.9 | convolution fusion | flops 402653184 | bytes 2490368 | tf_op jit(solution)/shard_map/dot_general | solution.py:41
  186.3 2.2 fusion.13
  188.5 2.2 fusion.15
  190.7 1.3 copy.110
  192.0 4.3 %fusion.1 = f32[1024,320]{0,1:T(8,128)S(1)} fusion(f32[2,1024,512]{2,1,0:T(8,128)} %all-gather.5.cloned.1.call-done, f32[2,512,320]{1,2,0:T(8,128)S(1)} %copy-done.4), kind=kOutput, calls=%fused_computation.8 | convolution fusion | flops 2013265920 | bytes 4063232 | tf_op jit(solution)/shard_map/dot_general | solution.py:41
  196.3 3.9 %fusion = f32[1024,320]{0,1:T(8,128)S(1)} fusion(f32[2,1024,512]{2,1,0:T(8,128)} %all-gather.5.cloned.1.call-done, f32[2,512,320]{1,2,0:T(8,128)S(1)} %copy-done.4), kind=kOutput, calls=%fused_computation.7 | convolution fusion | flops 2013265920 | bytes 4063232 | tf_op jit(solution)/shard_map/dot_general | solution.py:41
  200.3 2.4 fusion.9
  202.7 2.4 fusion.11
  205.1 1.7 pad_maximum_fusion.1
  206.8 2.3 copy.111
  209.1 5.5 %pad_maximum_fusion = f32[2,1024,896]{2,1,0:T(8,128)} fusion(f32[2,1024,320]{2,1,0:T(8,128)S(1)} %copy.111, f32[2,1024,64]{2,1,0:T(8,128)} %copy.110, f32[2,1024,512]{2,1,0:T(8,128)} %all-gather.5.cloned.1.call-done), kind=kLoop, calls=%fused_computation.2 | loop fusion | flops 3670016 | bytes 14680064 | tf_op jit(solution)/shard_map/concatenate | solution.py:91
  214.6 7.1 %gather_fusion.1 = f32[8,2,128,896]{3,2,1,0:T(8,128)} fusion(f32[2,8,128,896]{3,2,1,0:T(8,128)} %bitcast.116, s32[1024]{0:T(1024)S(1)} %pad_clamp_fusion), kind=kCustom, calls=%fused_computation.1 | custom fusion | bytes 14680096 | tf_op jit(solution)/shard_map/jit(_take)/gather | solution.py:67
  221.7 3.8 %copy.112 = f32[2,8,128,896]{3,2,1,0:T(8,128)S(1)} copy(f32[2,8,128,896]{3,2,0,1:T(8,128)} %bitcast.115) | data formatting | bytes 14680064 | tf_op jit(solution)/shard_map/jit(_take)/gather | solution.py:67
  225.5 0.6 bitcast_select_fusion
  226.0 2.9 %copy-done.2 = f32[2,1024,896]{2,1,0:T(8,128)} copy-done((f32[2,1024,896]{2,1,0:T(8,128)}, f32[2,1024,896]{2,1,0:T(8,128)S(1)}, u32[]{:S(2)}) %copy-start.2) | copy-done | bytes 7340056
  229.0 0.2 concatenate.8
  229.2 1.9 copy.113
  231.1 3.9 %all-to-all-start.1 = ((f32[2,2,512,384]{3,2,1,0:T(8,128)}), f32[2,2,512,384]{3,2,1,0:T(8,128)S(1)}, u32[]{:S(2)}, u32[]{:S(2)}) async-start(f32[2,2,512,384]{3,2,1,0:T(8,128)} %copy.113), calls=%async_computation.1 | async-start | bytes 6291456 | tf_op jit(solution)/shard_map/all_to_all | solution.py:25
  235.2 2.2 slice-done
  237.4 0.7 constant_dynamic-slice_fusion
  238.1 25.5 %all-to-all-done.1 = f32[2,2,512,384]{3,2,1,0:T(8,128)S(1)} async-done(((f32[2,2,512,384]{3,2,1,0:T(8,128)}), f32[2,2,512,384]{3,2,1,0:T(8,128)S(1)}, u32[]{:S(2)}, u32[]{:S(2)}) %all-to-all-start.1) | async-done | bytes 3145760 | tf_op jit(solution)/shard_map/all_to_all | solution.py:25
  263.6 1.5 reduce_sum.35
  265.1 1.9 split.9
  267.0 1.5 copy.116
  268.5 1.1 slice_add_fusion
  269.6 0.9 copy.115
  (35 shorter events, 0.9 us)
Async XLA Ops:
  7.2 79.9 %all-gather.3.cloned.1.call-start = ((), (), s32[]{:S(2)}) async-start(), calls=%async_computation.2 | async-start | bytes 2228224 | tf_op jit(solution)/shard_map/all_gather | solution.py:84
  7.9 170.8 %all-gather.5.cloned.1.call-start = ((), (), s32[]{:S(2)}) async-start(), calls=%async_computation.3 | async-start | bytes 4456448 | tf_op jit(solution)/shard_map/all_gather | solution.py:90
  7.9 15.8 %collective-permute-start = (f32[2,64,1024]{2,1,0:T(8,128)}, f32[2,64,1024]{2,1,0:T(8,128)S(1)}, u32[]{:S(2)}, u32[]{:S(2)}) collective-permute-start(f32[2,64,1024]{2,1,0:T(8,128)} %bitcast.121), channel_id=1, source_target_pairs={{0,16},{16,0},{1,17},{17,1},{2,18},{18,2},{3,19},{19,3},{4,20},{20... | collective-permute-start | bytes 1572872 | tf_op jit(solution)/shard_map/ppermute | solution.py:14
  87.1 4.8 %copy-start.3 = (f32[1,2,512,512]{2,3,1,0:T(8,128)S(1)}, f32[1,2,512,512]{2,3,1,0:T(8,128)}, u32[]{:S(2)}) copy-start(f32[1,2,512,512]{2,3,1,0:T(8,128)} %all-gather.3.cloned.1.call-done) | copy-start | bytes 6291460
  91.9 3.0 %copy-start.5 = (f32[1,2,64,1024]{3,2,1,0:T(8,128)S(1)}, f32[1,2,64,1024]{3,2,1,0:T(8,128)}, u32[]{:S(2)}) copy-start(f32[1,2,64,1024]{3,2,1,0:T(8,128)} %param.4) | copy-start | bytes 1572868
  95.0 10.5 %copy-start.6 = (s32[2,8]{1,0:T(2,128)S(1)}, s32[2,8]{1,0:T(2,128)}, u32[]{:S(2)}) copy-start(s32[2,8]{1,0:T(2,128)} %param.7) | copy-start | bytes 196
  97.5 32.6 %all-to-all-start = ((f32[16,1,8192]{2,1,0:T(1,128)}), f32[16,1,8192]{2,1,0:T(1,128)S(1)}, u32[]{:S(2)}, u32[]{:S(2)}) async-start(f32[16,1,8192]{2,1,0:T(1,128)} %reshape.137), calls=%async_computation | async-start | bytes 1048576 | tf_op jit(solution)/shard_map/all_to_all | solution.py:86
  178.7 7.6 %copy-start = (f32[2,1024,512]{2,1,0:T(8,128)S(1)}, f32[2,1024,512]{2,1,0:T(8,128)}, u32[]{:S(2)}) copy-start(f32[2,1024,512]{2,1,0:T(8,128)} %all-gather.5.cloned.1.call-done) | copy-start | bytes 12582916
  188.5 3.5 %copy-start.4 = (f32[2,512,320]{1,2,0:T(8,128)S(1)}, f32[2,512,320]{1,2,0:T(8,128)}, u32[]{:S(2)}) copy-start(f32[2,512,320]{1,2,0:T(8,128)} %param.6) | copy-start | bytes 3932164
  192.0 8.3 %copy-start.1 = (f32[2,1024,512]{2,1,0:T(8,128)S(1)}, f32[2,1024,512]{2,1,0:T(8,128)}, u32[]{:S(2)}) copy-start(f32[2,1024,512]{2,1,0:T(8,128)} %all-gather.5.cloned.1.call-done) | copy-start | bytes 12582916
  226.0 2.9 %copy-start.2 = (f32[2,1024,896]{2,1,0:T(8,128)}, f32[2,1024,896]{2,1,0:T(8,128)S(1)}, u32[]{:S(2)}) copy-start(f32[2,1024,896]{2,1,0:T(8,128)S(1)} %bitcast_select_fusion) | copy-start | bytes 22020100
  231.1 32.5 %all-to-all-start.1 = ((f32[2,2,512,384]{3,2,1,0:T(8,128)}), f32[2,2,512,384]{3,2,1,0:T(8,128)S(1)}, u32[]{:S(2)}, u32[]{:S(2)}) async-start(f32[2,2,512,384]{3,2,1,0:T(8,128)} %copy.113), calls=%async_computation.1 | async-start | bytes 6291456 | tf_op jit(solution)/shard_map/all_to_all | solution.py:25
  235.2 2.2 slice-start
Sparse Core Ops, SparseCore 0:
  10.1 76.9 all-gather.2
  95.0 83.6 all-gather.4
where the time goes:
time: 278 us; the launch traced here: 277 us
  waiting for transfers between devices  169 us (61%)
  local copies, waits for them, and re-layouts  32.3 us (12%)
  matrix products  32 us (12%)
  starting transfers between devices  15.5 us (6%)
  between operations  14.4 us (5%)
  other arithmetic  14.3 us (5%)
    all_gather x1, waiting for transfers between devices, per_device(): lax.all_gather(pivot_inverses, 'grp', axis=3, tiled=True)[0]  62.4 us
    all_gather x1, waiting for transfers between devices, per_device(): piece = lax.all_gather(raw_multipliers, 'grp', axis=1, tiled=True)  43.9 us
    dot_general x12, matrix products, product(): jnp.dot(first_part, second_part, precision=lax.Precision.HIGHEST, preferr...  32 us
    all_to_all x1, waiting for transfers between devices, summed_on_arrival(): lax.all_to_all(pieces, axis, split_axis=0, concat_axis=0, tiled=True)  25.5 us
    all_to_all x1, waiting for transfers between devices, per_device(): lax.all_to_all(beta_rows, 'grp', split_axis=2, concat_axis=1, tiled=True)  24.2 us
    ppermute x1, waiting for transfers between devices, partner(): return lax.ppermute(block, axis, route)  12.3 us
    gather x4, local copies, waits for them, and re-layouts, reorder(): return jnp.take(grouped, source, axis=1).reshape(matrix.shape)  11.5 us
    unnamed x18, local copies, waits for them, and re-layouts  8.03 us
  transfers between devices with their start and end apart: 5, of which 5 were waited for; matrix products, arithmetic and copies ran while one was open for 3% of the time, Pallas kernels for 0%

commit v1 on v0

--- a/solution.py
+++ b/solution.py
@@ -2,6 +2,13 @@
 import jax.numpy as jnp
 from jax import lax
 from jax.sharding import PartitionSpec as P
+
+perform_heaps = lambda local_array, axis_tag: jnp.concatenate(
+    lax.all_to_all(
+        jnp.stack([local_array for _ in range(lax.axis_size(axis_tag))]), axis_tag, 0, 0
+    ),
+    axis=3,
+)
 
 
 def partner(block, axis, bit):
@@ -80,9 +87,7 @@
     half_rows = order_size // 2
     to_beta, to_alpha = block_sources(face_blocks)
     panel_section = lax.dynamic_slice_in_dim(alpha_rows, sibling * panel_width, panel_width, 2)
-    raw_multipliers = complex_dot(
-        panel_section, lax.all_gather(pivot_inverses, "grp", axis=3, tiled=True)[0]
-    )
+    raw_multipliers = complex_dot(panel_section, perform_heaps(pivot_inverses, "grp")[0])
     beta_cols = lax.all_to_all(beta_rows, "grp", split_axis=2, concat_axis=1, tiled=True)
     beta_perm = reorder(beta_cols, to_alpha)
     local_cols = beta_perm.shape[2]

time: 278 us -> 318 us (1.14)
  the two profiles are of different devices: /device:TPU:4 before, /device:TPU:22 now
where the time goes in v1:
time: 318 us; the launch traced here: 317 us
  waiting for transfers between devices  195 us (61%)
  local copies, waits for them, and re-layouts  35.2 us (11%)
  starting transfers between devices  30.1 us (9%)
  matrix products  29.5 us (9%)
  between operations  14.4 us (5%)
  other arithmetic  13.4 us (4%)
    all_to_all x1, waiting for transfers between devices, lax.all_to_all(jnp.stack([local_array for _ in range(lax.axis_size(axis_t...  80 us
    all_gather x1, waiting for transfers between devices, per_device(): piece = lax.all_gather(raw_multipliers, 'grp', axis=1, tiled=True)  43.2 us
    all_to_all x1, waiting for transfers between devices, per_device(): lax.all_to_all(beta_rows, 'grp', split_axis=2, concat_axis=1, tiled=True)  33.7 us
    dot_general x12, matrix products, product(): jnp.dot(first_part, second_part, precision=lax.Precision.HIGHEST, preferr...  29.5 us
    all_to_all x1, waiting for transfers between devices, summed_on_arrival(): lax.all_to_all(pieces, axis, split_axis=0, concat_axis=0, tiled=True)  25.8 us
    all_to_all x1, starting transfers between devices, lax.all_to_all(jnp.stack([local_array for _ in range(lax.axis_size(axis_t...  15.3 us
    ppermute x1, waiting for transfers between devices, partner(): return lax.ppermute(block, axis, route)  12.1 us
    gather x4, local copies, waits for them, and re-layouts, reorder(): return jnp.take(grouped, source, axis=1).reshape(matrix.shape)  11.5 us
  transfers between devices with their start and end apart: 5, of which 5 were waited for; matrix products, arithmetic and copies ran while one was open for 3% of the time, Pallas kernels for 0%

profile of v1, /device:TPU:22, one launch (start us, length us, event | category | flops | bytes accessed | tf_op | source)
XLA Modules:
  0.0 317.4 jit_solution(5088917410621433626)
XLA Ops:
  7.2 2.5 stack.26
  9.7 15.3 %all-to-all-start = ((f32[16,1,2,512,32]{3,4,2,1,0:T(8,128)}), f32[16,1,2,512,32]{3,4,2,1,0:T(8,128)S(1)}, u32[]{:S(2)}, u32[]{:S(2)}) async-start(f32[16,1,2,512,32]{3,4,2,1,0:T(8,128)} %stack.26), calls=%async_computation | async-start | bytes 4194304 | tf_op jit(solution)/shard_map/all_to_all | solution.py:7
  25.1 3.2 %collective-permute-start = (f32[2,64,1024]{2,1,0:T(8,128)S(1)}, f32[2,64,1024]{2,1,0:T(8,128)S(1)}, u32[]{:S(2)}, u32[]{:S(2)}) collective-permute-start(f32[2,64,1024]{2,1,0:T(8,128)S(1)} %bitcast.128), channel_id=1, source_target_pairs={{0,16},{16,0},{1,17},{17,1},{2,18},{18,2},{3,19},{19,3},{4,20},{20... | collective-permute-start | bytes 1572872 | tf_op jit(solution)/shard_map/ppermute | solution.py:21
  28.3 12.1 %collective-permute-done = f32[2,64,1024]{2,1,0:T(8,128)S(1)} collective-permute-done((f32[2,64,1024]{2,1,0:T(8,128)S(1)}, f32[2,64,1024]{2,1,0:T(8,128)S(1)}, u32[]{:S(2)}, u32[]{:S(2)}) %collective-permute-start) | collective-permute-done | bytes 524320 | tf_op jit(solution)/shard_map/ppermute | solution.py:21
  40.4 80.0 %all-to-all-done = f32[16,1,2,512,32]{3,4,2,1,0:T(8,128)S(1)} async-done(((f32[16,1,2,512,32]{3,4,2,1,0:T(8,128)}), f32[16,1,2,512,32]{3,4,2,1,0:T(8,128)S(1)}, u32[]{:S(2)}, u32[]{:S(2)}) %all-to-all-start) | async-done | bytes 2097184 | tf_op jit(solution)/shard_map/all_to_all | solution.py:7
  120.4 0.2 copy.130
  120.6 0.3 fusion.30
  120.9 1.1 fusion.27
  122.0 1.1 fusion.26
  123.1 1.1 fusion.17
  124.3 1.1 fusion.16
  125.4 0.7 pad_maximum_fusion.2
  126.2 0.6 copy.112
  126.8 1.9 reshape.144
  128.7 7.6 %all-to-all-start.1 = ((f32[16,1,8192]{2,1,0:T(1,128)}), f32[16,1,8192]{2,1,0:T(1,128)S(1)}, u32[]{:S(2)}, u32[]{:S(2)}) async-start(f32[16,1,8192]{2,1,0:T(1,128)} %reshape.144), calls=%async_computation.1 | async-start | bytes 1048576 | tf_op jit(solution)/shard_map/all_to_all | solution.py:91
  136.7 33.7 %all-to-all-done.1 = f32[16,1,8192]{2,1,0:T(1,128)S(1)} async-done(((f32[16,1,8192]{2,1,0:T(1,128)}), f32[16,1,8192]{2,1,0:T(1,128)S(1)}, u32[]{:S(2)}, u32[]{:S(2)}) %all-to-all-start.1) | async-done | bytes 524320 | tf_op jit(solution)/shard_map/all_to_all | solution.py:91
  170.4 0.5 broadcast.135
  171.0 1.9 reduce
  172.9 0.8 reshape.145
  173.6 0.6 copy.131
  174.6 0.6 gather_fusion
  175.2 43.2 %all-gather.2.cloned.1.call-done = f32[2,1024,512]{2,1,0:T(8,128)} async-done(((f32[2,64,512]{2,1,0:T(8,128)}), f32[2,1024,512]{2,1,0:T(8,128)}) %all-gather.2.cloned.1.call-update) | async-done | bytes 4194320 | tf_op jit(solution)/shard_map/all_gather | solution.py:95
  218.4 3.9 %fusion.3 = f32[1024,64]{0,1:T(8,128)S(1)} fusion(f32[2,1024,512]{2,1,0:T(8,128)} %all-gather.2.cloned.1.call-done, f32[2,512,64]{1,2,0:T(8,128)S(1)} %dynamic-slice_select_fusion), kind=kOutput, calls=%fused_computation.11 | convolution fusion | flops 402653184 | bytes 2490368 | tf_op jit(solution)/shard_map/dot_general | solution.py:48
  222.3 3.7 %fusion.2 = f32[1024,64]{0,1:T(8,128)S(1)} fusion(f32[2,1024,512]{2,1,0:T(8,128)} %all-gather.2.cloned.1.call-done, f32[2,512,64]{1,2,0:T(8,128)S(1)} %dynamic-slice_select_fusion), kind=kOutput, calls=%fused_computation.10 | convolution fusion | flops 402653184 | bytes 2490368 | tf_op jit(solution)/shard_map/dot_general | solution.py:48
  226.0 2.2 fusion.13
  228.2 2.2 fusion.15
  230.4 1.3 copy.116
  231.7 4.3 %fusion.1 = f32[1024,320]{0,1:T(8,128)S(1)} fusion(f32[2,1024,512]{2,1,0:T(8,128)} %all-gather.2.cloned.1.call-done, f32[2,512,320]{1,2,0:T(8,128)S(1)} %copy-done.3), kind=kOutput, calls=%fused_computation.9 | convolution fusion | flops 2013265920 | bytes 4063232 | tf_op jit(solution)/shard_map/dot_general | solution.py:48
  236.1 3.9 %fusion = f32[1024,320]{0,1:T(8,128)S(1)} fusion(f32[2,1024,512]{2,1,0:T(8,128)} %all-gather.2.cloned.1.call-done, f32[2,512,320]{1,2,0:T(8,128)S(1)} %copy-done.3), kind=kOutput, calls=%fused_computation.8 | convolution fusion | flops 2013265920 | bytes 4063232 | tf_op jit(solution)/shard_map/dot_general | solution.py:48
  240.0 2.4 fusion.9
  242.4 2.4 fusion.11
  244.8 1.7 pad_maximum_fusion.1
  246.5 2.3 copy.117
  248.8 5.5 %pad_maximum_fusion = f32[2,1024,896]{2,1,0:T(8,128)} fusion(f32[2,1024,320]{2,1,0:T(8,128)S(1)} %copy.117, f32[2,1024,64]{2,1,0:T(8,128)} %copy.116, f32[2,1024,512]{2,1,0:T(8,128)} %all-gather.2.cloned.1.call-done), kind=kLoop, calls=%fused_computation.2 | loop fusion | flops 3670016 | bytes 14680064 | tf_op jit(solution)/shard_map/concatenate | solution.py:96
  254.3 7.1 %gather_fusion.1 = f32[8,2,128,896]{3,2,1,0:T(8,128)} fusion(f32[2,8,128,896]{3,2,1,0:T(8,128)} %bitcast.118, s32[1024]{0:T(1024)S(1)} %pad_clamp_fusion), kind=kCustom, calls=%fused_computation.1 | custom fusion | bytes 14680096 | tf_op jit(solution)/shard_map/jit(_take)/gather | solution.py:74
  261.4 3.8 %copy.118 = f32[2,8,128,896]{3,2,1,0:T(8,128)S(1)} copy(f32[2,8,128,896]{3,2,0,1:T(8,128)} %bitcast.117) | data formatting | bytes 14680064 | tf_op jit(solution)/shard_map/jit(_take)/gather | solution.py:74
  265.2 0.6 bitcast_select_fusion
  265.8 2.9 copy-done.2
  268.9 1.9 copy.119
  270.8 3.9 %all-to-all-start.2 = ((f32[2,2,512,384]{3,2,1,0:T(8,128)}), f32[2,2,512,384]{3,2,1,0:T(8,128)S(1)}, u32[]{:S(2)}, u32[]{:S(2)}) async-start(f32[2,2,512,384]{3,2,1,0:T(8,128)} %copy.119), calls=%async_computation.2 | async-start | bytes 6291456 | tf_op jit(solution)/shard_map/all_to_all | solution.py:32
  274.9 2.2 slice-done
  277.1 0.7 constant_dynamic-slice_fusion
  277.8 25.8 %all-to-all-done.2 = f32[2,2,512,384]{3,2,1,0:T(8,128)S(1)} async-done(((f32[2,2,512,384]{3,2,1,0:T(8,128)}), f32[2,2,512,384]{3,2,1,0:T(8,128)S(1)}, u32[]{:S(2)}, u32[]{:S(2)}) %all-to-all-start.2) | async-done | bytes 3145760 | tf_op jit(solution)/shard_map/all_to_all | solution.py:32
  303.6 1.5 reduce_sum.35
  305.1 1.9 split.9
  307.0 1.5 copy.122
  308.5 1.1 slice_add_fusion
  309.6 0.9 copy.121
  (35 shorter events, 1.3 us)
Async XLA Ops:
  9.7 15.4 %copy-start.4 = (f32[1,2,64,1024]{3,2,1,0:T(8,128)S(1)}, f32[1,2,64,1024]{3,2,1,0:T(8,128)}, u32[]{:S(2)}) copy-start(f32[1,2,64,1024]{3,2,1,0:T(8,128)} %param.4) | copy-start | bytes 1572868
  9.7 110.7 %all-to-all-start = ((f32[16,1,2,512,32]{3,4,2,1,0:T(8,128)}), f32[16,1,2,512,32]{3,4,2,1,0:T(8,128)S(1)}, u32[]{:S(2)}, u32[]{:S(2)}) async-start(f32[16,1,2,512,32]{3,4,2,1,0:T(8,128)} %stack.26), calls=%async_computation | async-start | bytes 4194304 | tf_op jit(solution)/shard_map/all_to_all | solution.py:7
  25.0 193.4 %all-gather.2.cloned.1.call-start = ((), (), s32[]{:S(2)}) async-start(), calls=%async_computation.3 | async-start | bytes 4456448 | tf_op jit(solution)/shard_map/all_gather | solution.py:95
  25.1 15.3 %collective-permute-start = (f32[2,64,1024]{2,1,0:T(8,128)S(1)}, f32[2,64,1024]{2,1,0:T(8,128)S(1)}, u32[]{:S(2)}, u32[]{:S(2)}) collective-permute-start(f32[2,64,1024]{2,1,0:T(8,128)S(1)} %bitcast.128), channel_id=1, source_target_pairs={{0,16},{16,0},{1,17},{17,1},{2,18},{18,2},{3,19},{19,3},{4,20},{20... | collective-permute-start | bytes 1572872 | tf_op jit(solution)/shard_map/ppermute | solution.py:21
  126.2 10.1 %copy-start.5 = (s32[2,8]{1,0:T(2,128)S(1)}, s32[2,8]{1,0:T(2,128)}, u32[]{:S(2)}) copy-start(s32[2,8]{1,0:T(2,128)} %param.7) | copy-start | bytes 196
  128.7 41.8 %all-to-all-start.1 = ((f32[16,1,8192]{2,1,0:T(1,128)}), f32[16,1,8192]{2,1,0:T(1,128)S(1)}, u32[]{:S(2)}, u32[]{:S(2)}) async-start(f32[16,1,8192]{2,1,0:T(1,128)} %reshape.144), calls=%async_computation.1 | async-start | bytes 1048576 | tf_op jit(solution)/shard_map/all_to_all | solution.py:91
  218.4 7.6 %copy-start = (f32[2,1024,512]{2,1,0:T(8,128)S(1)}, f32[2,1024,512]{2,1,0:T(8,128)}, u32[]{:S(2)}) copy-start(f32[2,1024,512]{2,1,0:T(8,128)} %all-gather.2.cloned.1.call-done) | copy-start | bytes 12582916
  228.2 3.5 %copy-start.3 = (f32[2,512,320]{1,2,0:T(8,128)S(1)}, f32[2,512,320]{1,2,0:T(8,128)}, u32[]{:S(2)}) copy-start(f32[2,512,320]{1,2,0:T(8,128)} %param.6) | copy-start | bytes 3932164
  231.7 8.3 %copy-start.1 = (f32[2,1024,512]{2,1,0:T(8,128)S(1)}, f32[2,1024,512]{2,1,0:T(8,128)}, u32[]{:S(2)}) copy-start(f32[2,1024,512]{2,1,0:T(8,128)} %all-gather.2.cloned.1.call-done) | copy-start | bytes 12582916
  265.8 2.9 copy-start.2
  270.8 32.8 %all-to-all-start.2 = ((f32[2,2,512,384]{3,2,1,0:T(8,128)}), f32[2,2,512,384]{3,2,1,0:T(8,128)S(1)}, u32[]{:S(2)}, u32[]{:S(2)}) async-start(f32[2,2,512,384]{3,2,1,0:T(8,128)} %copy.119), calls=%async_computation.2 | async-start | bytes 6291456 | tf_op jit(solution)/shard_map/all_to_all | solution.py:32
  274.9 2.2 slice-start
Sparse Core Ops, SparseCore 0:
  126.3 92.1 all-gather.1
